TPU v7x, 32 devices: a whole 2x2x4 slice. The times are simulated.
32 devices in a mesh: par: 4 (over x, core), freq: 8 (over z, y).
Axes of the slice: x: 2, y: 2, z: 4, core: 2. Of those that a mesh axis runs over, the one named last changes fastest.
Arguments:
- probes: bfloat16 [64, 600, 420], P('freq'), may hold values from -6 to 6
- map_real: bfloat16 [112, 600, 1024], P('freq', None, 'par'), may hold values from -0.1875 to 0.1875
- map_imag: bfloat16 [112, 600, 1024], P('freq', None, 'par'), may hold values from -0.1875 to 0.1875
- prior_var: float32 [1024], P('par'), may hold values from 0.05 to 13, as said below
Outputs:
- applied: bfloat16 [64, 600, 420], P('freq')
Inputs may be any that keep to these rules, and one draw needn't show every extreme that they name: `prior_var`: prior variances are positive.
All inputs are finite; a program needn't handle non-finite values.
Results may differ from a plain program's by a relative error of at most 0.014.
Values may be sent and summed in bfloat16 or wider, within the bound.
A program may use at most 64 MiB of HBM per device.

v0:
```python
import jax
import jax.numpy as jnp
from jax import lax
from jax.sharding import PartitionSpec as P

SENSORS = 600
STEPS = 420
PERIOD = 840
PROBES = 64
noise_ratio = 0.5


def split_product(left, table):
    upper = table.astype(jnp.bfloat16)
    lower = (table - upper.astype(jnp.float32)).astype(jnp.bfloat16)
    return jnp.dot(left, upper, preferred_element_type=jnp.float32) + jnp.dot(
        left, lower, preferred_element_type=jnp.float32
    )


def shards(probes, map_real, map_imag, prior_var):
    freq_count = lax.axis_size("freq")
    bins_dev = map_real.shape[0]
    probe_block = probes.shape[0]
    total_bins = bins_dev * freq_count
    time_steps = jnp.arange(STEPS, dtype=jnp.int32)
    bin_index = jnp.arange(total_bins, dtype=jnp.int32)
    product_index = time_steps[:, None] * bin_index[None, :] % PERIOD
    angles = product_index.astype(jnp.float32) * (2.0 * jnp.pi / PERIOD)
    norm_scale = 1.0 / jnp.sqrt(jnp.float32(PERIOD))
    cosines = jnp.cos(angles) * norm_scale
    sines = jnp.sin(angles) * norm_scale
    forward = jnp.stack([cosines, -sines], axis=2).reshape(STEPS, 2 * total_bins)
    all_weight = jnp.where(bin_index == 0, 1.0, 2.0).astype(jnp.float32)
    inverse = jnp.stack([cosines * all_weight[None, :], -sines * all_weight[None, :]], axis=2)
    inverse = inverse.reshape(STEPS, 2 * total_bins).T
    flattened = probes.reshape(probe_block * SENSORS, STEPS)
    spectrum = split_product(flattened, forward).astype(jnp.bfloat16)
    spectrum = spectrum.reshape(probe_block, SENSORS, 2 * total_bins)
    exchanged = lax.all_to_all(spectrum, "freq", split_axis=2, concat_axis=0, tiled=True)
    all_probes = exchanged.shape[0]
    operand = exchanged.reshape(all_probes, SENSORS, bins_dev, 2).transpose(2, 1, 3, 0)
    operand = operand.reshape(bins_dev, SENSORS, 2 * all_probes)
    left_real = jnp.einsum("ksp,ksc->kpc", map_real, operand, preferred_element_type=jnp.float32)
    left_imag = jnp.einsum("ksp,ksc->kpc", map_imag, operand, preferred_element_type=jnp.float32)
    u_real = left_real[..., :all_probes] + left_imag[..., all_probes:]
    u_imag = left_real[..., all_probes:] - left_imag[..., :all_probes]
    global_bin = lax.axis_index("freq") * bins_dev + jnp.arange(bins_dev, dtype=jnp.int32)
    bin_weight = jnp.where(global_bin == 0, 1.0, 2.0).astype(jnp.float32)
    quadratic = jnp.sum(
        bin_weight[:, None, None] * prior_var[None, :, None] * (u_real * u_real + u_imag * u_imag)
    )
    trace_est = lax.psum(quadratic, ("par", "freq")) / (PROBES * SENSORS * STEPS)
    scaled = (jnp.concatenate([u_real, u_imag], axis=-1) * prior_var[None, :, None]).astype(
        jnp.bfloat16
    )
    right_real = jnp.einsum("ksp,kpc->ksc", map_real, scaled, preferred_element_type=jnp.float32)
    right_imag = jnp.einsum("ksp,kpc->ksc", map_imag, scaled, preferred_element_type=jnp.float32)
    w_partial = jnp.concatenate(
        [
            right_real[..., :all_probes] - right_imag[..., all_probes:],
            right_real[..., all_probes:] + right_imag[..., :all_probes],
        ],
        axis=-1,
    )
    summed = lax.psum(w_partial.astype(jnp.bfloat16), "par")
    outgoing = summed.reshape(bins_dev, SENSORS, 2, all_probes).transpose(3, 1, 0, 2)
    outgoing = outgoing.reshape(all_probes, SENSORS, 2 * bins_dev)
    by_probe = lax.all_to_all(outgoing, "freq", split_axis=0, concat_axis=2, tiled=True)
    by_rows = by_probe.reshape(probe_block * SENSORS, 2 * total_bins)
    response = split_product(by_rows, inverse).reshape(probe_block, SENSORS, STEPS)
    return (response + noise_ratio * trace_est * probes.astype(jnp.float32)).astype(jnp.bfloat16)


def solution(mesh):
    placed = (P("freq", None, None), P("freq", None, "par"), P("freq", None, "par"), P("par"))
    return jax.shard_map(
        shards, mesh=mesh, in_specs=placed, out_specs=P("freq", None, None), check_vma=False
    )
```

profile of v0, /device:TPU:0, one launch (start us, length us, event | category | flops | bytes accessed | tf_op | source)
XLA Modules:
  0.0 288.2 jit_solution(12911080688204210552)
XLA Ops:
  6.5 7.8 %multiply_negate_fusion = (f32[420,112,1]{0,2,1:T(1,128)S(1)}, f32[420,112,1]{0,2,1:T(1,128)S(1)}) fusion(), kind=kLoop, calls=%fused_computation.29 | loop fusion | flops 564480 | bytes 376320 | tf_op jit(solution)/shard_map/neg | solution.py:33
  14.4 0.5 subtract_convert_fusion
  14.8 0.4 fusion.9
  15.3 0.2 convert_element_type.96
  15.5 0.2 convert_element_type.99
  15.7 8.0 %reshape.201 = bf16[4800,420]{0,1:T(8,128)(2,1)} reshape(bf16[8,600,420]{1,0,2:T(8,128)(2,1)} %param.4) | data formatting | bytes 8064000 | tf_op jit(solution)/shard_map/reshape | solution.py:37
  23.6 0.0 copy-start
  23.6 3.6 %fusion.20 = f32[224,4800]{1,0:T(8,128)S(1)} fusion(bf16[420,224]{0,1:T(8,128)(2,1)S(1)} %convert_element_type.96, bf16[4800,420]{0,1:T(8,128)(2,1)} %reshape.201), kind=kOutput, calls=%fused_computation.44 | convolution fusion | flops 903168000 | bytes 8520960 | tf_op jit(solution)/shard_map/dot_general | solution.py:16
  27.2 0.0 copy-done
  27.3 1.3 fusion.1
  28.6 0.0 copy-start.1
  28.6 3.8 %reshape.202 = bf16[8,600,224]{1,0,2:T(8,128)(2,1)} reshape(bf16[4800,224]{0,1:T(8,128)(2,1)S(1)} %fusion.1) | data formatting | bytes 4300800 | tf_op jit(solution)/shard_map/reshape | solution.py:39
  32.4 0.0 slice-start.2
  32.4 7.4 %all-to-all-start = ((bf16[8,600,224]{1,0,2:T(8,128)(2,1)}), bf16[8,600,224]{1,0,2:T(8,128)(2,1)S(1)}, u32[]{:S(2)}, u32[]{:S(2)}) async-start(bf16[8,600,224]{1,0,2:T(8,128)(2,1)} %reshape.202), calls=%async_computation | async-start | bytes 4587520 | tf_op jit(solution)/shard_map/all_to_all | solution.py:40
  39.9 0.2 all-reduce.2.cloned.1.call-start
  40.1 0.0 copy-done.1
  40.1 0.1 broadcast_multiply_fusion.3
  40.2 52.1 %all-to-all-done = bf16[8,600,224]{1,0,2:T(8,128)(2,1)S(1)} async-done(((bf16[8,600,224]{1,0,2:T(8,128)(2,1)}), bf16[8,600,224]{1,0,2:T(8,128)(2,1)S(1)}, u32[]{:S(2)}, u32[]{:S(2)}) %all-to-all-start) | async-done | bytes 2150432 | tf_op jit(solution)/shard_map/all_to_all | solution.py:40
  92.3 0.3 copy.20
  92.7 0.0 slice-start
  92.7 3.3 %convolution_bitcast_fusion.2 = f32[14,256,128]{1,2,0:T(8,128)S(1)} fusion(bf16[14,600,128]{1,2,0:T(8,128)(2,1)S(1)} %bitcast.74, bf16[14,600,256]{2,1,0:T(8,128)(2,1)} %param.6), kind=kOutput, calls=%fused_computation.15 | convolution fusion | flops 550502400 | bytes 8286208 | tf_op jit(solution)/shard_map/ksp,ksc->kpc/dot_general | solution.py:45
  96.0 0.0 slice-done.2
  96.0 0.0 slice-done.3
  96.0 0.0 slice-start.1
  96.0 0.9 convolution_bitcast_fusion.3
  97.0 1.1 multiply_reduce_fusion
  98.1 0.0 slice-done
  98.1 0.0 slice-done.1
  98.1 1.3 convolution_bitcast_fusion
  99.4 1.3 convolution_bitcast_fusion.1
  100.7 2.4 fusion.3
  103.2 1.2 pad_maximum_fusion
  104.4 3.4 %copy.25 = bf16[14,600,128]{1,2,0:T(8,128)(2,1)} copy(bf16[14,600,128]{2,1,0:T(8,128)(2,1)S(1)} %pad_maximum_fusion) | data formatting | bytes 4300800 | tf_op jit(solution)/shard_map/concatenate | solution.py:59
  107.7 0.0 all-reduce.2.cloned.1.call-update
  107.8 53.8 %all-reduce.2.cloned.1.call-done = bf16[64,600,28]{1,0,2:T(8,128)(2,1)} async-done(((bf16[64,600,28]{1,0,2:T(8,128)(2,1)}), bf16[64,600,28]{1,0,2:T(8,128)(2,1)}) %all-reduce.2.cloned.1.call-update) | async-done | bytes 2150416 | tf_op jit(solution)/shard_map/psum | solution.py:66
  161.6 4.5 %copy.26 = bf16[64,600,28]{1,2,0:T(8,128)(2,1)} copy(bf16[64,600,28]{1,0,2:T(8,128)(2,1)} %all-reduce.2.cloned.1.call-done) | data formatting | bytes 4300800 | tf_op jit(solution)/shard_map/psum | solution.py:66
  166.0 5.5 %all-to-all-start.1 = ((bf16[64,600,28]{1,2,0:T(8,128)(2,1)}), bf16[64,600,28]{1,2,0:T(8,128)(2,1)S(1)}, u32[]{:S(2)}, u32[]{:S(2)}) async-start(bf16[64,600,28]{1,2,0:T(8,128)(2,1)} %copy.26), calls=%async_computation.1 | async-start | bytes 5242880 | tf_op jit(solution)/shard_map/all_to_all | solution.py:69
  171.6 8.0 %broadcast_multiply_fusion = (f32[420,112,1]{0,2,1:T(1,128)S(1)}, f32[420,112,1]{0,2,1:T(1,128)S(1)}) fusion(f32[112]{0:T(128)S(1)} %compare_select_fusion.1, f32[112]{0:T(128)S(1)} %broadcast_multiply_fusion.4), kind=kLoop, calls=%fused_computation.31 | loop fusion | flops 611520 | bytes 377216 | tf_op jit(solution)/shard_map/mul | solution.py:35
  179.6 0.4 pad_maximum_fusion.2
  180.1 0.3 reshape.208
  180.4 70.5 %psum.15 = f32[]{:T(128)} all-reduce(f32[]{:T(128)} %get-tuple-element.5), channel_id=1, replica_groups=mesh['par'=4,'freq'=8] {'par','freq'}, use_global_device_ids=true, to_apply=%region_2.3 | all-reduce | flops 1 | bytes 8 | tf_op jit(solution)/shard_map/psum | solution.py:53
  251.5 0.0 all-to-all-done.1
  251.5 2.2 copy.33
  253.8 3.6 %reshape.207 = bf16[4800,224]{0,1:T(8,128)(2,1)S(1)} reshape(bf16[8,600,8,28]{1,0,3,2:T(8,128)(2,1)} %bitcast.83) | data formatting | bytes 4300800 | tf_op jit(solution)/shard_map/reshape | solution.py:70
  257.4 1.3 fusion.17
  258.6 4.6 %convolution_add_fusion = f32[4800,420]{0,1:T(8,128)} fusion(f32[4800,420]{0,1:T(8,128)S(1)} %fusion.17, bf16[4800,224]{0,1:T(8,128)(2,1)S(1)} %reshape.207, f32[420,224]{0,1:T(8,128)S(1)} %reshape.208), kind=kOutput, calls=%fused_computation.1 | convolution fusion | flops 905560320 | bytes 18654720 | tf_op jit(solution)/shard_map/dot_general | solution.py:16
  263.2 10.4 %reshape.209 = f32[8,600,420]{1,0,2:T(8,128)} reshape(f32[4800,420]{0,1:T(8,128)} %convolution_add_fusion) | data formatting | bytes 16128000 | tf_op jit(solution)/shard_map/reshape | solution.py:71
  273.6 7.7 %add_convert_fusion = bf16[8,600,420]{1,0,2:T(8,128)(2,1)} fusion(f32[8,600,420]{1,0,2:T(8,128)} %reshape.209, bf16[8,600,420]{1,0,2:T(8,128)(2,1)} %param.4, f32[]{:T(128)S(6)} %mul_shard_map.3), kind=kLoop, calls=%fused_computation | loop fusion | flops 8064000 | bytes 16128004 | tf_op jit(solution)/shard_map/convert_element_type | solution.py:72
  (6 shorter events, 0.0 us)
Async XLA Ops:
  23.6 3.6 %copy-start = (bf16[4800,420]{0,1:T(8,128)(2,1)S(1)}, bf16[4800,420]{0,1:T(8,128)(2,1)}, u32[]{:S(2)}) copy-start(bf16[4800,420]{0,1:T(8,128)(2,1)} %reshape.201) | copy-start | bytes 12096004
  28.6 11.5 %copy-start.1 = (f32[256]{0:T(256)S(1)}, f32[256]{0:T(256)}, u32[]{:S(2)}) copy-start(f32[256]{0:T(256)} %param.7) | copy-start | bytes 3076
  32.4 63.6 %slice-start.2 = ((s8[4300800]{0:T(1024)(128)(4,1)}), s8[106496]{0:T(1024)(128)(4,1)S(1)}, s32[]{:S(2)}) async-start(s8[4300800]{0:T(1024)(128)(4,1)} %bitcast.78), calls=%async_computation.5 | async-start | bytes 212992
  32.4 59.9 %all-to-all-start = ((bf16[8,600,224]{1,0,2:T(8,128)(2,1)}), bf16[8,600,224]{1,0,2:T(8,128)(2,1)S(1)}, u32[]{:S(2)}, u32[]{:S(2)}) async-start(bf16[8,600,224]{1,0,2:T(8,128)(2,1)} %reshape.202), calls=%async_computation | async-start | bytes 4587520 | tf_op jit(solution)/shard_map/all_to_all | solution.py:40
  39.9 121.7 %all-reduce.2.cloned.1.call-start = ((), (), s32[]{:S(2)}) async-start(), calls=%async_computation.2 | async-start | bytes 4587520 | tf_op jit(solution)/shard_map/psum | solution.py:66
  92.3 3.7 %slice-start.3 = ((s8[4300800]{0:T(1024)(128)(4,1)}), s8[4194304]{0:T(1024)(128)(4,1)S(1)}, s32[]{:S(2)}) async-start(s8[4300800]{0:T(1024)(128)(4,1)} %bitcast.78), calls=%async_computation.6 | async-start | bytes 8388608
  92.7 5.4 %slice-start = ((s8[4300800]{0:T(1024)(128)(4,1)}), s8[4194304]{0:T(1024)(128)(4,1)S(1)}, s32[]{:S(2)}) async-start(s8[4300800]{0:T(1024)(128)(4,1)} %bitcast.76), calls=%async_computation.3 | async-start | bytes 8388608
  96.0 2.0 slice-start.1
  166.0 85.5 %all-to-all-start.1 = ((bf16[64,600,28]{1,2,0:T(8,128)(2,1)}), bf16[64,600,28]{1,2,0:T(8,128)(2,1)S(1)}, u32[]{:S(2)}, u32[]{:S(2)}) async-start(bf16[64,600,28]{1,2,0:T(8,128)(2,1)} %copy.26), calls=%async_computation.1 | async-start | bytes 5242880 | tf_op jit(solution)/shard_map/all_to_all | solution.py:69
Sparse Core Ops, SparseCore 0:
  107.9 53.6 all-reduce.1
where the time goes:
time: 289 us; the launch traced here: 288 us
  waiting for transfers between devices  106 us (37%)
  blocking collectives  70.5 us (24%)
  local copies, waits for them, and re-layouts  36.9 us (13%)
  other arithmetic  29.7 us (10%)
  matrix products  17.7 us (6%)
  between operations  14.3 us (5%)
  starting transfers between devices  13.2 us (5%)
    psum x1, blocking collectives, shards(): lax.psum(quadratic, ('par', 'freq')) / (PROBES * SENSORS * STEPS)  70.5 us
    psum x1, waiting for transfers between devices, shards(): summed = lax.psum(w_partial.astype(jnp.bfloat16), 'par')  53.8 us
    all_to_all x1, waiting for transfers between devices, shards(): lax.all_to_all(spectrum, 'freq', split_axis=2, concat_axis=0, tiled=True)  52.1 us
    reshape x1, local copies, waits for them, and re-layouts, shards(): split_product(by_rows, inverse).reshape(probe_block, SENSORS, STEPS)  10.4 us
    mul x1, other arithmetic, shards(): -sines * all_weight[None, :]  8.04 us
    reshape x1, local copies, waits for them, and re-layouts, shards(): flattened = probes.reshape(probe_block * SENSORS, STEPS)  7.96 us
    neg x1, other arithmetic, shards(): -sines  7.81 us
    convert_element_type x1, other arithmetic, shards(): (response + noise_ratio * trace_est * probes.astype(jnp.float32)).astype(...  7.71 us
  transfers between devices with their start and end apart: 3, of which 2 were waited for; matrix products, arithmetic and copies ran while one was open for 3% of the time, Pallas kernels for 0%

commit v1 on v0

--- a/solution.py
+++ b/solution.py
@@ -63,7 +63,7 @@
         ],
         axis=-1,
     )
-    summed = lax.psum(w_partial.astype(jnp.bfloat16), "par")
+    summed = jnp.sum(lax.all_gather(w_partial.astype(jnp.bfloat16), "par"), axis=0)
     outgoing = summed.reshape(bins_dev, SENSORS, 2, all_probes).transpose(3, 1, 0, 2)
     outgoing = outgoing.reshape(all_probes, SENSORS, 2 * bins_dev)
     by_probe = lax.all_to_all(outgoing, "freq", split_axis=0, concat_axis=2, tiled=True)

time: 289 us -> 301 us (1.042)
  other arithmetic: 29.7 us -> 37.7 us
  waiting for transfers between devices: 106 us -> 111 us
    all_gather x0 -> x1, waiting for transfers between devices: none -> 58.7 us  [shards(): lax.all_gather(w_partial.astype(jnp.bfloat16), 'par')]
    psum x1 -> x0, waiting for transfers between devices: 53.8 us -> none  [shards(): summed = lax.psum(w_partial.astype(jnp.bfloat16), 'par')]
    reduce_sum x0 -> x1, other arithmetic: none -> 6.65 us  [shards(): jnp.sum(lax.all_gather(w_partial.astype(jnp.bfloat16), 'par'), axis=0)]
    psum x1 -> x0, local copies, waits for them, and re-layouts: 4.46 us -> none  [shards(): summed = lax.psum(w_partial.astype(jnp.bfloat16), 'par')]
    concatenate x1 -> x2, other arithmetic: 1.18 us -> 4.96 us  [shards(): jnp.concatenate([right_real[..., :all_probes] - right_imag[..., all_probe...]
    concatenate x1 -> x0, local copies, waits for them, and re-layouts: 3.37 us -> none  [shards(): jnp.concatenate([right_real[..., :all_probes] - right_imag[..., all_probe...]
    reduce_sum x0 -> x1, local copies, waits for them, and re-layouts: none -> 3.27 us  [shards(): jnp.sum(lax.all_gather(w_partial.astype(jnp.bfloat16), 'par'), axis=0)]
where the time goes in v1:
time: 301 us; the launch traced here: 300 us
  waiting for transfers between devices  111 us (37%)
  blocking collectives  71.2 us (24%)
  other arithmetic  37.7 us (13%)
  local copies, waits for them, and re-layouts  35.1 us (12%)
  matrix products  17.7 us (6%)
  between operations  14.3 us (5%)
  starting transfers between devices  13.2 us (4%)
    psum x1, blocking collectives, shards(): lax.psum(quadratic, ('par', 'freq')) / (PROBES * SENSORS * STEPS)  71.2 us
    all_gather x1, waiting for transfers between devices, shards(): lax.all_gather(w_partial.astype(jnp.bfloat16), 'par')  58.7 us
    all_to_all x1, waiting for transfers between devices, shards(): lax.all_to_all(spectrum, 'freq', split_axis=2, concat_axis=0, tiled=True)  52.1 us
    reshape x1, local copies, waits for them, and re-layouts, shards(): split_product(by_rows, inverse).reshape(probe_block, SENSORS, STEPS)  10.4 us
    mul x1, other arithmetic, shards(): -sines * all_weight[None, :]  8.04 us
    reshape x1, local copies, waits for them, and re-layouts, shards(): flattened = probes.reshape(probe_block * SENSORS, STEPS)  7.96 us
    neg x1, other arithmetic, shards(): -sines  7.81 us
    convert_element_type x1, other arithmetic, shards(): (response + noise_ratio * trace_est * probes.astype(jnp.float32)).astype(...  7.71 us
  transfers between devices with their start and end apart: 3, of which 2 were waited for; matrix products, arithmetic and copies ran while one was open for 3% of the time, Pallas kernels for 0%

profile of v1, /device:TPU:0, one launch (start us, length us, event | category | flops | bytes accessed | tf_op | source)
XLA Modules:
  0.0 300.0 jit_solution(15637428624718160441)
XLA Ops:
  6.5 7.8 %multiply_negate_fusion = (f32[420,112,1]{0,2,1:T(1,128)S(1)}, f32[420,112,1]{0,2,1:T(1,128)S(1)}) fusion(), kind=kLoop, calls=%fused_computation.31 | loop fusion | flops 564480 | bytes 376320 | tf_op jit(solution)/shard_map/neg | solution.py:33
  14.4 0.5 subtract_convert_fusion
  14.8 0.4 fusion.11
  15.3 0.2 convert_element_type.105
  15.5 0.2 convert_element_type.108
  15.7 8.0 %reshape.232 = bf16[4800,420]{0,1:T(8,128)(2,1)} reshape(bf16[8,600,420]{1,0,2:T(8,128)(2,1)} %param.4) | data formatting | bytes 8064000 | tf_op jit(solution)/shard_map/reshape | solution.py:37
  23.6 0.0 copy-start
  23.6 3.6 %fusion.22 = f32[224,4800]{1,0:T(8,128)S(1)} fusion(bf16[420,224]{0,1:T(8,128)(2,1)S(1)} %convert_element_type.105, bf16[4800,420]{0,1:T(8,128)(2,1)} %reshape.232), kind=kOutput, calls=%fused_computation.46 | convolution fusion | flops 903168000 | bytes 8520960 | tf_op jit(solution)/shard_map/dot_general | solution.py:16
  27.2 0.0 copy-done
  27.3 1.3 fusion.1
  28.6 0.0 copy-start.1
  28.6 3.8 %reshape.233 = bf16[8,600,224]{1,0,2:T(8,128)(2,1)} reshape(bf16[4800,224]{0,1:T(8,128)(2,1)S(1)} %fusion.1) | data formatting | bytes 4300800 | tf_op jit(solution)/shard_map/reshape | solution.py:39
  32.4 7.4 %all-to-all-start = ((bf16[8,600,224]{1,0,2:T(8,128)(2,1)}), bf16[8,600,224]{1,0,2:T(8,128)(2,1)S(1)}, u32[]{:S(2)}, u32[]{:S(2)}) async-start(bf16[8,600,224]{1,0,2:T(8,128)(2,1)} %reshape.233), calls=%async_computation | async-start | bytes 4587520 | tf_op jit(solution)/shard_map/all_to_all | solution.py:40
  39.9 0.2 all-gather.2.cloned.1.call-start
  40.1 0.0 copy-done.1
  40.1 0.1 broadcast_multiply_fusion.3
  40.2 52.1 %all-to-all-done = bf16[8,600,224]{1,0,2:T(8,128)(2,1)S(1)} async-done(((bf16[8,600,224]{1,0,2:T(8,128)(2,1)}), bf16[8,600,224]{1,0,2:T(8,128)(2,1)S(1)}, u32[]{:S(2)}, u32[]{:S(2)}) %all-to-all-start) | async-done | bytes 2150432 | tf_op jit(solution)/shard_map/all_to_all | solution.py:40
  92.3 0.3 copy.18
  92.7 0.0 slice-start
  92.7 3.3 %convolution_bitcast_fusion.2 = f32[14,256,128]{1,2,0:T(8,128)S(1)} fusion(bf16[14,600,128]{1,2,0:T(8,128)(2,1)S(1)} %bitcast.78, bf16[14,600,256]{2,1,0:T(8,128)(2,1)} %param.6), kind=kOutput, calls=%fused_computation.17 | convolution fusion | flops 550502400 | bytes 8286208 | tf_op jit(solution)/shard_map/ksp,ksc->kpc/dot_general | solution.py:45
  96.0 0.0 slice-done.2
  96.0 0.0 slice-done.3
  96.0 0.0 slice-start.1
  96.0 0.9 convolution_bitcast_fusion.3
  97.0 1.0 multiply_reduce_fusion
  98.0 0.0 slice-done
  98.0 0.0 slice-done.1
  98.0 1.3 convolution_bitcast_fusion
  99.4 1.3 convolution_bitcast_fusion.1
  100.7 2.4 fusion.4
  103.2 2.5 pad_maximum_fusion
  105.7 0.0 all-gather.2.cloned.1.call-update
  105.7 58.7 %all-gather.2.cloned.1.call-done = bf16[4,14,600,128]{3,2,1,0:T(8,128)(2,1)} async-done(((bf16[1,14,600,128]{3,2,1,0:T(8,128)(2,1)}), bf16[4,14,600,128]{3,2,1,0:T(8,128)(2,1)}) %all-gather.2.cloned.1.call-update) | async-done | bytes 8601616 | tf_op jit(solution)/shard_map/all_gather | solution.py:66
  164.4 6.7 %reduce_sum.21 = bf16[14,600,128]{2,1,0:T(8,128)(2,1)} reduce(bf16[4,14,600,128]{3,2,1,0:T(8,128)(2,1)} %all-gather.2.cloned.1.call-done, bf16[]{:T(256)} %constant.15.clone.1), dimensions={0}, to_apply=%region_0.1 | reduce | flops 3225600 | bytes 10752002 | tf_op jit(solution)/shard_map/reduce_sum | solution.py:66
  171.0 3.3 %copy.23 = bf16[14,600,128]{1,2,0:T(8,128)(2,1)S(1)} copy(bf16[14,600,128]{2,1,0:T(8,128)(2,1)} %reduce_sum.21) | data formatting | bytes 4300800 | tf_op jit(solution)/shard_map/reduce_sum | solution.py:66
  174.3 2.8 copy.24
  177.1 5.5 %all-to-all-start.1 = ((bf16[64,600,28]{1,2,0:T(8,128)(2,1)}), bf16[64,600,28]{1,2,0:T(8,128)(2,1)S(1)}, u32[]{:S(2)}, u32[]{:S(2)}) async-start(bf16[64,600,28]{1,2,0:T(8,128)(2,1)} %copy.24), calls=%async_computation.1 | async-start | bytes 5242880 | tf_op jit(solution)/shard_map/all_to_all | solution.py:69
  182.7 8.0 %broadcast_multiply_fusion = (f32[420,112,1]{0,2,1:T(1,128)S(1)}, f32[420,112,1]{0,2,1:T(1,128)S(1)}) fusion(f32[112]{0:T(128)S(1)} %compare_select_fusion.1, f32[112]{0:T(128)S(1)} %broadcast_multiply_fusion.4), kind=kLoop, calls=%fused_computation.33 | loop fusion | flops 611520 | bytes 377216 | tf_op jit(solution)/shard_map/mul | solution.py:35
  190.7 0.4 pad_maximum_fusion.2
  191.2 0.3 reshape.239
  191.5 71.2 %psum.7 = f32[]{:T(128)} all-reduce(f32[]{:T(128)} %get-tuple-element.5), channel_id=1, replica_groups=mesh['par'=4,'freq'=8] {'par','freq'}, use_global_device_ids=true, to_apply=%region_2.3 | all-reduce | flops 1 | bytes 8 | tf_op jit(solution)/shard_map/psum | solution.py:53
  263.3 0.0 all-to-all-done.1
  263.3 2.2 copy.31
  265.5 3.6 %reshape.238 = bf16[4800,224]{0,1:T(8,128)(2,1)S(1)} reshape(bf16[8,600,8,28]{1,0,3,2:T(8,128)(2,1)} %bitcast.87) | data formatting | bytes 4300800 | tf_op jit(solution)/shard_map/reshape | solution.py:70
  269.1 1.3 fusion.19
  270.4 4.6 %convolution_add_fusion = f32[4800,420]{0,1:T(8,128)} fusion(f32[4800,420]{0,1:T(8,128)S(1)} %fusion.19, bf16[4800,224]{0,1:T(8,128)(2,1)S(1)} %reshape.238, f32[420,224]{0,1:T(8,128)S(1)} %reshape.239), kind=kOutput, calls=%fused_computation.1 | convolution fusion | flops 905560320 | bytes 18654720 | tf_op jit(solution)/shard_map/dot_general | solution.py:16
  275.0 10.4 %reshape.240 = f32[8,600,420]{1,0,2:T(8,128)} reshape(f32[4800,420]{0,1:T(8,128)} %convolution_add_fusion) | data formatting | bytes 16128000 | tf_op jit(solution)/shard_map/reshape | solution.py:71
  285.4 7.7 %add_convert_fusion = bf16[8,600,420]{1,0,2:T(8,128)(2,1)} fusion(f32[8,600,420]{1,0,2:T(8,128)} %reshape.240, bf16[8,600,420]{1,0,2:T(8,128)(2,1)} %param.4, f32[]{:T(128)S(6)} %mul_shard_map.3), kind=kLoop, calls=%fused_computation | loop fusion | flops 8064000 | bytes 16128004 | tf_op jit(solution)/shard_map/convert_element_type | solution.py:72
  (7 shorter events, 0.0 us)
Async XLA Ops:
  23.6 3.6 %copy-start = (bf16[4800,420]{0,1:T(8,128)(2,1)S(1)}, bf16[4800,420]{0,1:T(8,128)(2,1)}, u32[]{:S(2)}) copy-start(bf16[4800,420]{0,1:T(8,128)(2,1)} %reshape.232) | copy-start | bytes 12096004
  28.6 11.5 %copy-start.1 = (f32[256]{0:T(256)S(1)}, f32[256]{0:T(256)}, u32[]{:S(2)}) copy-start(f32[256]{0:T(256)} %param.7) | copy-start | bytes 3076
  32.4 63.6 %slice-start.2 = ((s8[4300800]{0:T(1024)(128)(4,1)}), s8[106496]{0:T(1024)(128)(4,1)S(1)}, s32[]{:S(2)}) async-start(s8[4300800]{0:T(1024)(128)(4,1)} %bitcast.82), calls=%async_computation.5 | async-start | bytes 212992
  32.4 59.9 %all-to-all-start = ((bf16[8,600,224]{1,0,2:T(8,128)(2,1)}), bf16[8,600,224]{1,0,2:T(8,128)(2,1)S(1)}, u32[]{:S(2)}, u32[]{:S(2)}) async-start(bf16[8,600,224]{1,0,2:T(8,128)(2,1)} %reshape.233), calls=%async_computation | async-start | bytes 4587520 | tf_op jit(solution)/shard_map/all_to_all | solution.py:40
  39.9 124.5 %all-gather.2.cloned.1.call-start = ((), (), s32[]{:S(2)}) async-start(), calls=%async_computation.2 | async-start | bytes 10752000 | tf_op jit(solution)/shard_map/all_gather | solution.py:66
  92.3 3.7 %slice-start.3 = ((s8[4300800]{0:T(1024)(128)(4,1)}), s8[4194304]{0:T(1024)(128)(4,1)S(1)}, s32[]{:S(2)}) async-start(s8[4300800]{0:T(1024)(128)(4,1)} %bitcast.82), calls=%async_computation.6 | async-start | bytes 8388608
  92.7 5.4 %slice-start = ((s8[4300800]{0:T(1024)(128)(4,1)}), s8[4194304]{0:T(1024)(128)(4,1)S(1)}, s32[]{:S(2)}) async-start(s8[4300800]{0:T(1024)(128)(4,1)} %bitcast.80), calls=%async_computation.3 | async-start | bytes 8388608
  96.0 2.0 slice-start.1
  177.1 86.2 %all-to-all-start.1 = ((bf16[64,600,28]{1,2,0:T(8,128)(2,1)}), bf16[64,600,28]{1,2,0:T(8,128)(2,1)S(1)}, u32[]{:S(2)}, u32[]{:S(2)}) async-start(bf16[64,600,28]{1,2,0:T(8,128)(2,1)} %copy.24), calls=%async_computation.1 | async-start | bytes 5242880 | tf_op jit(solution)/shard_map/all_to_all | solution.py:69
Sparse Core Ops, SparseCore 0:
  105.8 58.5 all-gather.1
